TPU v7x, 32 devices: a whole 2x2x4 slice. The times are simulated.
32 devices in a mesh: rows: 4 (over y, x), batch: 8 (over z, core).
Axes of the slice: x: 2, y: 2, z: 4, core: 2. Of those that a mesh axis runs over, the one named last changes fastest.
Arguments:
- control: bfloat16 [8, 24, 96, 320], P('batch', 'rows'), may hold values from -60 to 60, as said below
- unet_skips: bfloat16 [2, 8, 24, 96, 320], P(None, 'batch', 'rows'), may hold values from -6 to 6
- norm_gains: float32 [2, 2, 320], replicated, may hold values from 0.25 to 1.75
- norm_shifts: float32 [2, 2, 320], replicated, may hold values from -3 to 3
- conv_weights: bfloat16 [2, 2, 3, 960, 320], P(None, None, None, None, 'batch'), may hold values from -0.109375 to 0.109375
- zero_weights: bfloat16 [2, 1, 320, 320], P(None, None, None, 'batch'), may hold values from -0.3125 to 0.3125
Outputs:
- controls: bfloat16 [2, 8, 24, 96, 320], P(None, 'batch', 'rows')
Inputs may be any that keep to these rules, and one draw needn't show every extreme that they name: `control`: Real-valued latent features.
All inputs are finite; a program needn't handle non-finite values.
Results may differ from a plain program's by a relative error of at most 0.01.
Values may be sent and summed in bfloat16 or wider, within the bound.
A program may use at most 64 MiB of HBM per device.

v0:
```python
import jax
import jax.numpy as jnp
from jax import lax
from jax.sharding import PartitionSpec as P

GROUPS = 32


epsilon = 1e-05


def extended(block, sides, width):
    for axis, dim in sides:
        count = lax.axis_size(axis)
        forward = [(i, i + 1) for i in range(count - 1)]
        backward = [(target, source) for source, target in forward]
        low = lax.ppermute(
            lax.slice_in_dim(block, block.shape[dim] - width, None, axis=dim), axis, forward
        )
        high = lax.ppermute(lax.slice_in_dim(block, 0, width, axis=dim), axis, backward)
        block = jnp.concatenate([low, block, high], axis=dim)
    return block


def normalize(values, gain_row, shift_row):
    samples, height, across, channels = values.shape
    members = height * lax.axis_size("rows") * across * (channels // GROUPS)
    grouped = values.astype(jnp.float32).reshape(
        samples, height, across, GROUPS, channels // GROUPS
    )
    partial_sum, partial_square = lax.psum(
        (
            jnp.sum(grouped, axis=(1, 2, 4), keepdims=True),
            jnp.sum(grouped * grouped, axis=(1, 2, 4), keepdims=True),
        ),
        "rows",
    )
    average = partial_sum / members
    spread = partial_square / members - average * average
    centered = grouped - average
    scaled = (centered * lax.rsqrt(spread + epsilon)).reshape(
        samples, height, across, channels
    ) * gain_row + shift_row
    return jax.nn.silu(scaled).astype(jnp.bfloat16)


def apply_taps(padded, weight_piece):
    tap_rows = weight_piece.shape[0]
    tap_cols = weight_piece.shape[1] // padded.shape[3]
    height = padded.shape[1] - tap_rows + 1
    across = padded.shape[2] - tap_cols + 1
    summed = jnp.zeros((padded.shape[0], height, across, weight_piece.shape[2]), jnp.float32)
    for row_tap in range(tap_rows):
        row_band = padded[:, row_tap : row_tap + height]
        if tap_cols > 1:
            stacked = jnp.concatenate(
                [row_band[:, :, col_tap : col_tap + across] for col_tap in range(tap_cols)], axis=3
            )
        else:
            stacked = row_band
        summed = summed + jnp.einsum(
            "bhwk,kc->bhwc", stacked, weight_piece[row_tap], preferred_element_type=jnp.float32
        )
    return summed


def convolve(values, weight):
    if weight.shape[0] > 1:
        padded = extended(values, (("rows", 1),), 1)
        padded = jnp.pad(padded, ((0, 0), (0, 0), (1, 1), (0, 0)))
    else:
        padded = values
    complete = lax.all_gather(weight, "batch", axis=2, tiled=True)
    return apply_taps(padded, complete)


def on_device(control, unet_skips, norm_gains, norm_shifts, conv_weights, zero_weights):
    hidden = control
    results = []
    for layer_index in range(conv_weights.shape[0]):
        normed = normalize(hidden, norm_gains[layer_index, 0], norm_shifts[layer_index, 0])
        first = convolve(normed, conv_weights[layer_index, 0]).astype(jnp.bfloat16)
        normed_two = normalize(first, norm_gains[layer_index, 1], norm_shifts[layer_index, 1])
        second = convolve(normed_two, conv_weights[layer_index, 1])
        hidden = (hidden.astype(jnp.float32) + second).astype(jnp.bfloat16)
        zeroed = convolve(hidden, zero_weights[layer_index])
        results.append((zeroed + unet_skips[layer_index].astype(jnp.float32)).astype(jnp.bfloat16))
    return jnp.stack(results)


def solution(mesh):
    placed = (
        P("batch", "rows", None, None),
        P(None, "batch", "rows", None, None),
        P(),
        P(),
        P(None, None, None, None, "batch"),
        P(None, None, None, "batch"),
    )
    return jax.shard_map(
        on_device,
        mesh=mesh,
        in_specs=placed,
        out_specs=P(None, "batch", "rows", None, None),
        check_vma=False,
    )
```

profile of v0, /device:TPU:0, one launch (start us, length us, event | category | flops | bytes accessed | tf_op | source)
XLA Modules:
  0.0 152.8 jit_solution(14512298526885135947)
XLA Ops:
  6.6 2.3 %fusion.153 = (bf16[1,1,3,960,40]{3,4,2,1,0:T(8,128)(2,1)}, bf16[1,1,3,960,40]{3,4,2,1,0:T(8,128)(2,1)}, bf16[1,1,3,960,40]{3,4,2,1,0:T(8,128)(2,1)}, bf16[1,1,3,960,40]{3,4,2,1,0:T(8,128)(2,1)}) fusion(bf16[2,2,3,960,40]{3,4,2,1,0:T(8,128)(2,1)} %param.10), kind=kLoop, calls=%fused_computation.215 | loop fusion | bytes 1843200 | tf_op jit(solution)/shard_map/slice | solution.py:84
  11.1 11.4 %all-reduce.7 = (f32[1,1,1,32,1]{3,4,2,1,0:T(1,128)S(1)}, f32[1,1,1,32,1]{3,4,2,1,0:T(1,128)S(1)}) all-reduce(f32[1,1,1,32,1]{3,4,2,1,0:T(1,128)S(1)} %bitcast.189, f32[1,1,1,32,1]{3,4,2,1,0:T(1,128)S(1)} %bitcast.187), channel_id=1, replica_groups=mesh['rows'=4,'batch'=8] {'rows'}, use_global_device_ids=true, to_apply=%region_5.6 | all-reduce | flops 64 | bytes 512 | tf_op jit(solution)/shard_map/psum | solution.py:31
  23.8 2.2 %collective-permute-start = (bf16[1,1,96,320]{3,2,1,0:T(8,128)(2,1)S(1)}, bf16[1,1,96,320]{3,2,1,0:T(8,128)(2,1)}, u32[]{:S(2)}, u32[]{:S(2)}) collective-permute-start(bf16[1,1,96,320]{3,2,1,0:T(8,128)(2,1)S(1)} %get-tuple-element.64), channel_id=1, source_target_pairs={{0,8},{8,16},{16,24},{1,9},{9,17},{17,25},{2,10},{10,18},{18,26},{... | collective-permute-start | bytes 184328 | tf_op jit(solution)/shard_map/ppermute | solution.py:17
  26.0 1.3 collective-permute-start.1
  28.0 4.3 %collective-permute-done.1 = bf16[1,1,96,320]{3,2,1,0:T(8,128)(2,1)S(1)} collective-permute-done((bf16[1,1,96,320]{3,2,1,0:T(8,128)(2,1)S(1)}, bf16[1,1,96,320]{3,2,1,0:T(8,128)(2,1)S(1)}, u32[]{:S(2)}, u32[]{:S(2)}) %collective-permute-start.1) | collective-permute-done | bytes 61472 | tf_op jit(solution)/shard_map/ppermute | solution.py:20
  34.3 5.6 %all-gather.11.cloned.1.call-done = bf16[1,1,3,960,320]{3,4,2,1,0:T(8,128)(2,1)} async-done(((bf16[1,1,3,960,40]{3,4,2,1,0:T(8,128)(2,1)}), bf16[1,1,3,960,320]{3,4,2,1,0:T(8,128)(2,1)}) %all-gather.11.cloned.1.call-update) | async-done | bytes 1843216 | tf_op jit(solution)/shard_map/all_gather | solution.py:73
  39.9 2.0 %fusion.53 = f32[6,96,320]{2,1,0:T(8,128)S(1)} fusion(bf16[1,6,96,320]{3,2,1,0:T(8,128)(2,1)S(1)} %fusion.116, bf16[1,1,96,320]{3,2,1,0:T(8,128)(2,1)} %collective-permute-done, bf16[1,6,96,320]{3,2,1,0:T(8,128)(2,1)S(1)} %get-tuple-element.54, bf16[1,6,96,320]{3,2,1,0:T(8,128)(2,1)S(1)} %get-tuple-element.55, ...), kind=kOutput, calls=%fused_computation.80 | convolution fusion | flops 358318080 | bytes 2572288 | tf_op jit(solution)/shard_map/bhwk,kc->bhwc/dot_general | solution.py:61
  44.1 9.8 %all-reduce.6 = (f32[1,1,1,32,1]{3,4,2,1,0:T(1,128)S(1)}, f32[1,1,1,32,1]{3,4,2,1,0:T(1,128)S(1)}) all-reduce(f32[1,1,1,32,1]{3,4,2,1,0:T(1,128)S(1)} %bitcast.190, f32[1,1,1,32,1]{3,4,2,1,0:T(1,128)S(1)} %bitcast.185), channel_id=1, replica_groups=mesh['rows'=4,'batch'=8] {'rows'}, use_global_device_ids=true, to_apply=%region_11.12 | all-reduce | flops 64 | bytes 512 | tf_op jit(solution)/shard_map/psum | solution.py:31
  54.7 1.7 %collective-permute-start.2 = (bf16[1,1,96,320]{3,2,1,0:T(8,128)(2,1)S(1)}, bf16[1,1,96,320]{3,2,1,0:T(8,128)(2,1)S(1)}, u32[]{:S(2)}, u32[]{:S(2)}) collective-permute-start(bf16[1,1,96,320]{3,2,1,0:T(8,128)(2,1)S(1)} %get-tuple-element.62), channel_id=1, source_target_pairs={{0,8},{8,16},{16,24},{1,9},{9,17},{17,25},{2,10},{10,18},{18,26},{... | collective-permute-start | bytes 184328 | tf_op jit(solution)/shard_map/ppermute | solution.py:17
  56.4 1.3 collective-permute-start.3
  57.7 16.0 %all-gather.5 = bf16[1,1,320,320]{2,3,1,0:T(8,128)(2,1)} all-gather(bf16[1,1,320,40]{2,3,1,0:T(8,128)(2,1)S(1)} %copy-done.4), channel_id=7, replica_groups=mesh['rows'=4,'batch'=8] {'batch'}, dimensions={3}, use_global_device_ids=true | all-gather | bytes 230400 | tf_op jit(solution)/shard_map/all_gather | solution.py:73
  75.5 2.1 %fusion.42 = f32[6,96,320]{2,1,0:T(8,128)S(1)} fusion(bf16[1,6,96,320]{3,2,1,0:T(8,128)(2,1)S(1)} %fusion.136, bf16[1,1,96,320]{3,2,1,0:T(8,128)(2,1)} %copy-done.11, bf16[1,6,96,320]{3,2,1,0:T(8,128)(2,1)S(1)} %get-tuple-element.48, bf16[1,6,96,320]{3,2,1,0:T(8,128)(2,1)S(1)} %get-tuple-element.49, ...), kind=kOutput, calls=%fused_computation.69 | convolution fusion | flops 358318080 | bytes 2572288 | tf_op jit(solution)/shard_map/bhwk,kc->bhwc/dot_general | solution.py:61
  79.7 11.0 %all-reduce.5 = (f32[1,1,1,32,1]{3,4,2,1,0:T(1,128)S(1)}, f32[1,1,1,32,1]{3,4,2,1,0:T(1,128)S(1)}) all-reduce(f32[1,1,1,32,1]{3,4,2,1,0:T(1,128)S(1)} %bitcast.191, f32[1,1,1,32,1]{3,4,2,1,0:T(1,128)S(1)} %bitcast.186), channel_id=1, replica_groups=mesh['rows'=4,'batch'=8] {'rows'}, use_global_device_ids=true, to_apply=%region_17.18 | all-reduce | flops 64 | bytes 512 | tf_op jit(solution)/shard_map/psum | solution.py:31
  91.4 3.3 %collective-permute-start.4 = (bf16[1,1,96,320]{3,2,1,0:T(8,128)(2,1)S(1)}, bf16[1,1,96,320]{3,2,1,0:T(8,128)(2,1)S(1)}, u32[]{:S(2)}, u32[]{:S(2)}) collective-permute-start(bf16[1,1,96,320]{3,2,1,0:T(8,128)(2,1)S(1)} %get-tuple-element.60), channel_id=1, source_target_pairs={{0,8},{8,16},{16,24},{1,9},{9,17},{17,25},{2,10},{10,18},{18,26},{... | collective-permute-start | bytes 184328 | tf_op jit(solution)/shard_map/ppermute | solution.py:17
  94.8 1.3 collective-permute-start.5
  96.1 14.3 %all-gather.2 = bf16[1,1,320,320]{2,3,1,0:T(8,128)(2,1)S(1)} all-gather(bf16[1,1,320,40]{2,3,1,0:T(8,128)(2,1)S(1)} %copy-done.3), channel_id=4, replica_groups=mesh['rows'=4,'batch'=8] {'batch'}, dimensions={3}, use_global_device_ids=true | all-gather | bytes 230400 | tf_op jit(solution)/shard_map/all_gather | solution.py:73
  111.6 2.2 %fusion.31 = f32[6,96,320]{2,1,0:T(8,128)S(1)} fusion(bf16[1,6,96,320]{3,2,1,0:T(8,128)(2,1)S(1)} %fusion.126, bf16[1,1,96,320]{3,2,1,0:T(8,128)(2,1)S(1)} %collective-permute-done.4, bf16[1,6,96,320]{3,2,1,0:T(8,128)(2,1)S(1)} %get-tuple-element.42, bf16[1,6,96,320]{3,2,1,0:T(8,128)(2,1)} %get-tuple-element.43, ...), kind=kOutput, calls=%fused_computation.58 | convolution fusion | flops 358318080 | bytes 2633728 | tf_op jit(solution)/shard_map/bhwk,kc->bhwc/dot_general | solution.py:61
  115.9 11.1 %all-reduce.4 = (f32[1,1,1,32,1]{3,4,2,1,0:T(1,128)S(1)}, f32[1,1,1,32,1]{3,4,2,1,0:T(1,128)S(1)}) all-reduce(f32[1,1,1,32,1]{3,4,2,1,0:T(1,128)S(1)} %bitcast.188, f32[1,1,1,32,1]{3,4,2,1,0:T(1,128)S(1)} %bitcast.184), channel_id=1, replica_groups=mesh['rows'=4,'batch'=8] {'rows'}, use_global_device_ids=true, to_apply=%region_23.24 | all-reduce | flops 64 | bytes 512 | tf_op jit(solution)/shard_map/psum | solution.py:31
  127.7 1.9 %collective-permute-start.6 = (bf16[1,1,96,320]{3,2,1,0:T(8,128)(2,1)S(1)}, bf16[1,1,96,320]{3,2,1,0:T(8,128)(2,1)S(1)}, u32[]{:S(2)}, u32[]{:S(2)}) collective-permute-start(bf16[1,1,96,320]{3,2,1,0:T(8,128)(2,1)S(1)} %get-tuple-element.58), channel_id=1, source_target_pairs={{0,8},{8,16},{16,24},{1,9},{9,17},{17,25},{2,10},{10,18},{18,26},{... | collective-permute-start | bytes 184328 | tf_op jit(solution)/shard_map/ppermute | solution.py:17
  129.6 1.3 collective-permute-start.7
  131.6 4.3 %collective-permute-done.7 = bf16[1,1,96,320]{3,2,1,0:T(8,128)(2,1)S(1)} collective-permute-done((bf16[1,1,96,320]{3,2,1,0:T(8,128)(2,1)S(1)}, bf16[1,1,96,320]{3,2,1,0:T(8,128)(2,1)S(1)}, u32[]{:S(2)}, u32[]{:S(2)}) %collective-permute-start.7) | collective-permute-done | bytes 61472 | tf_op jit(solution)/shard_map/ppermute | solution.py:20
  137.7 2.0 %fusion.20 = f32[6,96,320]{2,1,0:T(8,128)S(1)} fusion(bf16[1,6,96,320]{3,2,1,0:T(8,128)(2,1)S(1)} %fusion.135, bf16[1,1,96,320]{3,2,1,0:T(8,128)(2,1)} %copy-done.12, bf16[1,6,96,320]{3,2,1,0:T(8,128)(2,1)S(1)} %get-tuple-element.36, bf16[1,6,96,320]{3,2,1,0:T(8,128)(2,1)} %get-tuple-element.37, bf16[1,1,3,960,320]{3,4,2,1,0:T(8,128)(2,1)} %all-gather.17.cloned.1.call-done), kind=kOutput, calls=%fused_computation.47 | convolution fusion | flops 358318080 | bytes 2646016 | tf_op jit(solution)/shard_map/bhwk,kc->bhwc/dot_general | solution.py:61
  139.8 2.8 %convolution_add_fusion.3 = f32[6,96,320]{2,1,0:T(8,128)} fusion(f32[6,96,320]{2,1,0:T(8,128)S(1)} %fusion.20, bf16[1,6,96,320]{3,2,1,0:T(8,128)(2,1)S(1)} %get-tuple-element.34, bf16[1,6,96,320]{3,2,1,0:T(8,128)(2,1)S(1)} %fusion.135, bf16[1,6,96,320]{3,2,1,0:T(8,128)(2,1)S(1)} %get-tuple-element.35, ...), kind=kOutput, calls=%fused_computation.20 | convolution fusion | flops 357396480 | bytes 3235840 | tf_op jit(solution)/shard_map/bhwk,kc->bhwc/dot_general | solution.py:61
  142.7 2.5 %fusion.9 = bf16[1,1,6,96,320]{4,3,2,1,0:T(8,128)(2,1)S(1)} fusion(f32[6,96,320]{2,1,0:T(8,128)} %convolution_add_fusion.3, bf16[1,6,96,320]{3,2,1,0:T(8,128)(2,1)S(1)} %get-tuple-element.76, bf16[1,1,96,320]{3,2,1,0:T(8,128)(2,1)S(1)} %copy-done.10, bf16[1,6,96,320]{3,2,1,0:T(8,128)(2,1)S(1)} %fusion.135, ...), kind=kOutput, calls=%fused_computation.35 | convolution fusion | flops 477573120 | bytes 4091904 | tf_op jit(solution)/shard_map/bhwk,kc->bhwc/dot_general | solution.py:61
  (122 shorter events, 21.3 us)
Async XLA Ops:
  6.5 3.9 %copy-start = (bf16[1,6,96,320]{3,2,1,0:T(8,128)(2,1)S(1)}, bf16[1,6,96,320]{3,2,1,0:T(8,128)(2,1)}, u32[]{:S(2)}) copy-start(bf16[1,6,96,320]{3,2,1,0:T(8,128)(2,1)} %param.6) | copy-start | bytes 1105924
  6.5 16.3 %copy-start.17 = (f32[2,2,320]{2,1,0:T(2,128)S(1)}, f32[2,2,320]{2,1,0:T(2,128)}, u32[]{:S(2)}) copy-start(f32[2,2,320]{2,1,0:T(2,128)} %param.8) | copy-start | bytes 15364
  6.5 16.3 %copy-start.16 = (f32[2,2,320]{2,1,0:T(2,128)S(1)}, f32[2,2,320]{2,1,0:T(2,128)}, u32[]{:S(2)}) copy-start(f32[2,2,320]{2,1,0:T(2,128)} %param.9) | copy-start | bytes 15364
  6.5 20.8 %copy-start.13 = (bf16[2,1,320,40]{2,3,1,0:T(8,128)(2,1)S(1)}, bf16[2,1,320,40]{2,3,1,0:T(8,128)(2,1)}, u32[]{:S(2)}) copy-start(bf16[2,1,320,40]{2,3,1,0:T(8,128)(2,1)} %param.11) | copy-start | bytes 153604
  6.5 33.3 %all-gather.11.cloned.1.call-start = ((), (), s32[]{:S(2)}) async-start(), calls=%async_computation | async-start | bytes 2211840 | tf_op jit(solution)/shard_map/all_gather | solution.py:73
  8.9 66.5 %all-gather.13.cloned.1.call-start = ((), (), s32[]{:S(2)}) async-start(), calls=%async_computation.1 | async-start | bytes 2211840 | tf_op jit(solution)/shard_map/all_gather | solution.py:73
  9.7 102.0 %all-gather.15.cloned.1.call-start = ((), (), s32[]{:S(2)}) async-start(), calls=%async_computation.2 | async-start | bytes 2211840 | tf_op jit(solution)/shard_map/all_gather | solution.py:73
  10.4 127.3 %all-gather.17.cloned.1.call-start = ((), (), s32[]{:S(2)}) async-start(), calls=%async_computation.3 | async-start | bytes 2211840 | tf_op jit(solution)/shard_map/all_gather | solution.py:73
  23.8 4.1 %collective-permute-start = (bf16[1,1,96,320]{3,2,1,0:T(8,128)(2,1)S(1)}, bf16[1,1,96,320]{3,2,1,0:T(8,128)(2,1)}, u32[]{:S(2)}, u32[]{:S(2)}) collective-permute-start(bf16[1,1,96,320]{3,2,1,0:T(8,128)(2,1)S(1)} %get-tuple-element.64), channel_id=1, source_target_pairs={{0,8},{8,16},{16,24},{1,9},{9,17},{17,25},{2,10},{10,18},{18,26},{... | collective-permute-start | bytes 184328 | tf_op jit(solution)/shard_map/ppermute | solution.py:17
  26.0 6.2 %collective-permute-start.1 = (bf16[1,1,96,320]{3,2,1,0:T(8,128)(2,1)S(1)}, bf16[1,1,96,320]{3,2,1,0:T(8,128)(2,1)S(1)}, u32[]{:S(2)}, u32[]{:S(2)}) collective-permute-start(bf16[1,1,96,320]{3,2,1,0:T(8,128)(2,1)S(1)} %get-tuple-element.63), channel_id=1, source_target_pairs={{8,0},{16,8},{24,16},{9,1},{17,9},{25,17},{10,2},{18,10},{26,18},{... | collective-permute-start | bytes 184328 | tf_op jit(solution)/shard_map/ppermute | solution.py:20
  42.8 11.5 %copy-start.14 = (f32[320]{0:T(512)S(1)}, f32[320]{0:T(512)}, u32[]{:S(2)}) copy-start(f32[320]{0:T(512)} %get-tuple-element.18) | copy-start | bytes 3844
  42.8 11.5 %copy-start.15 = (f32[320]{0:T(512)S(1)}, f32[320]{0:T(512)}, u32[]{:S(2)}) copy-start(f32[320]{0:T(512)} %get-tuple-element.80) | copy-start | bytes 3844
  42.8 14.9 %copy-start.4 = (bf16[1,1,320,40]{2,3,1,0:T(8,128)(2,1)S(1)}, bf16[1,1,320,40]{2,3,1,0:T(8,128)(2,1)}, u32[]{:S(2)}) copy-start(bf16[1,1,320,40]{2,3,1,0:T(8,128)(2,1)} %get-tuple-element.66) | copy-start | bytes 76804
  54.7 19.0 %collective-permute-start.2 = (bf16[1,1,96,320]{3,2,1,0:T(8,128)(2,1)S(1)}, bf16[1,1,96,320]{3,2,1,0:T(8,128)(2,1)S(1)}, u32[]{:S(2)}, u32[]{:S(2)}) collective-permute-start(bf16[1,1,96,320]{3,2,1,0:T(8,128)(2,1)S(1)} %get-tuple-element.62), channel_id=1, source_target_pairs={{0,8},{8,16},{16,24},{1,9},{9,17},{17,25},{2,10},{10,18},{18,26},{... | collective-permute-start | bytes 184328 | tf_op jit(solution)/shard_map/ppermute | solution.py:17
  56.4 17.3 %collective-permute-start.3 = (bf16[1,1,96,320]{3,2,1,0:T(8,128)(2,1)S(1)}, bf16[1,1,96,320]{3,2,1,0:T(8,128)(2,1)S(1)}, u32[]{:S(2)}, u32[]{:S(2)}) collective-permute-start(bf16[1,1,96,320]{3,2,1,0:T(8,128)(2,1)S(1)} %get-tuple-element.61), channel_id=1, source_target_pairs={{8,0},{16,8},{24,16},{9,1},{17,9},{25,17},{10,2},{18,10},{26,18},{... | collective-permute-start | bytes 184328 | tf_op jit(solution)/shard_map/ppermute | solution.py:20
  78.4 17.7 %copy-start.3 = (bf16[1,1,320,40]{2,3,1,0:T(8,128)(2,1)S(1)}, bf16[1,1,320,40]{2,3,1,0:T(8,128)(2,1)}, u32[]{:S(2)}) copy-start(bf16[1,1,320,40]{2,3,1,0:T(8,128)(2,1)} %get-tuple-element.65) | copy-start | bytes 76804
  91.4 19.0 %collective-permute-start.4 = (bf16[1,1,96,320]{3,2,1,0:T(8,128)(2,1)S(1)}, bf16[1,1,96,320]{3,2,1,0:T(8,128)(2,1)S(1)}, u32[]{:S(2)}, u32[]{:S(2)}) collective-permute-start(bf16[1,1,96,320]{3,2,1,0:T(8,128)(2,1)S(1)} %get-tuple-element.60), channel_id=1, source_target_pairs={{0,8},{8,16},{16,24},{1,9},{9,17},{17,25},{2,10},{10,18},{18,26},{... | collective-permute-start | bytes 184328 | tf_op jit(solution)/shard_map/ppermute | solution.py:17
  94.8 15.7 %collective-permute-start.5 = (bf16[1,1,96,320]{3,2,1,0:T(8,128)(2,1)S(1)}, bf16[1,1,96,320]{3,2,1,0:T(8,128)(2,1)S(1)}, u32[]{:S(2)}, u32[]{:S(2)}) collective-permute-start(bf16[1,1,96,320]{3,2,1,0:T(8,128)(2,1)S(1)} %get-tuple-element.59), channel_id=1, source_target_pairs={{8,0},{16,8},{24,16},{9,1},{17,9},{25,17},{10,2},{18,10},{26,18},{... | collective-permute-start | bytes 184328 | tf_op jit(solution)/shard_map/ppermute | solution.py:20
  114.6 16.3 %copy-start.2 = (bf16[2,1,6,96,320]{4,3,2,1,0:T(8,128)(2,1)S(1)}, bf16[2,1,6,96,320]{4,3,2,1,0:T(8,128)(2,1)}, u32[]{:S(2)}) copy-start(bf16[2,1,6,96,320]{4,3,2,1,0:T(8,128)(2,1)} %param.7) | copy-start | bytes 2211844
  127.7 3.8 %collective-permute-start.6 = (bf16[1,1,96,320]{3,2,1,0:T(8,128)(2,1)S(1)}, bf16[1,1,96,320]{3,2,1,0:T(8,128)(2,1)S(1)}, u32[]{:S(2)}, u32[]{:S(2)}) collective-permute-start(bf16[1,1,96,320]{3,2,1,0:T(8,128)(2,1)S(1)} %get-tuple-element.58), channel_id=1, source_target_pairs={{0,8},{8,16},{16,24},{1,9},{9,17},{17,25},{2,10},{10,18},{18,26},{... | collective-permute-start | bytes 184328 | tf_op jit(solution)/shard_map/ppermute | solution.py:17
  129.6 6.3 %collective-permute-start.7 = (bf16[1,1,96,320]{3,2,1,0:T(8,128)(2,1)S(1)}, bf16[1,1,96,320]{3,2,1,0:T(8,128)(2,1)S(1)}, u32[]{:S(2)}, u32[]{:S(2)}) collective-permute-start(bf16[1,1,96,320]{3,2,1,0:T(8,128)(2,1)S(1)} %get-tuple-element.57), channel_id=1, source_target_pairs={{8,0},{16,8},{24,16},{9,1},{17,9},{25,17},{10,2},{18,10},{26,18},{... | collective-permute-start | bytes 184328 | tf_op jit(solution)/shard_map/ppermute | solution.py:20
  131.6 4.3 %copy-start.12 = (bf16[1,1,96,320]{3,2,1,0:T(8,128)(2,1)}, bf16[1,1,96,320]{3,2,1,0:T(8,128)(2,1)S(1)}, u32[]{:S(2)}) copy-start(bf16[1,1,96,320]{3,2,1,0:T(8,128)(2,1)S(1)} %collective-permute-done.6) | copy-start | bytes 184324
  139.8 2.9 %copy-start.1 = (bf16[1,1,320,320]{2,3,1,0:T(8,128)(2,1)S(1)}, bf16[1,1,320,320]{2,3,1,0:T(8,128)(2,1)}, u32[]{:S(2)}) copy-start(bf16[1,1,320,320]{2,3,1,0:T(8,128)(2,1)} %all-gather.5) | copy-start | bytes 614404
  139.8 2.9 %copy-start.10 = (bf16[1,1,96,320]{3,2,1,0:T(8,128)(2,1)S(1)}, bf16[1,1,96,320]{3,2,1,0:T(8,128)(2,1)}, u32[]{:S(2)}) copy-start(bf16[1,1,96,320]{3,2,1,0:T(8,128)(2,1)} %copy-done.9) | copy-start | bytes 184324
  (9 other events, 10.6 us)
Sparse Core Ops, SparseCore 0:
  9.0 30.7 all-gather.10
  41.5 29.1 all-gather.12
  72.2 27.3 all-gather.14
  101.1 27.4 all-gather.16
where the time goes:
time: 154 us; the launch traced here: 153 us
  blocking collectives  73.5 us (48%)
  matrix products  19.1 us (12%)
  waiting for transfers between devices  15.9 us (10%)
  starting transfers between devices  14.4 us (9%)
  between operations  13.6 us (9%)
  local copies, waits for them, and re-layouts  11.2 us (7%)
  other arithmetic  5.14 us (3%)
    psum x4, blocking collectives, normalize(): lax.psum((jnp.sum(grouped, axis=(1, 2, 4), keepdims=True), jnp.sum(groupe...  43.2 us
    all_gather x2, blocking collectives, convolve(): complete = lax.all_gather(weight, 'batch', axis=2, tiled=True)  30.3 us
    dot_general x13, matrix products, apply_taps(): jnp.einsum('bhwk,kc->bhwc', stacked, weight_piece[row_tap], preferred_ele...  19.1 us
    ppermute x4, starting transfers between devices, extended(): lax.ppermute(lax.slice_in_dim(block, block.shape[dim] - width, None, axis...  9.07 us
    ppermute x4, waiting for transfers between devices, extended(): lax.ppermute(lax.slice_in_dim(block, 0, width, axis=dim), axis, backward)  8.61 us
    all_gather x4, waiting for transfers between devices, convolve(): complete = lax.all_gather(weight, 'batch', axis=2, tiled=True)  5.62 us
    ppermute x4, starting transfers between devices, extended(): lax.ppermute(lax.slice_in_dim(block, 0, width, axis=dim), axis, backward)  5.16 us
  transfers between devices with their start and end apart: 12, of which 4 were waited for; matrix products, arithmetic and copies ran while one was open for 14% of the time, Pallas kernels for 0%

commit v1 on v0

v1 whole, which is shorter than its diff:
```python
import functools

import jax
import jax.numpy as jnp
import numpy as np
from jax import lax
from jax.experimental import pallas as pl
from jax.experimental.pallas import tpu as pltpu
from jax.sharding import PartitionSpec as P

GROUPS = 32
EPSILON = 1e-05
MESH = pl.DeviceIdType.MESH


def layout_of(conv_weights):
    blocks, convs, taps, depth, outs = conv_weights.shape
    channels = depth // 3
    places = convs * (depth // channels)
    need = taps * outs + -(-outs // places)
    lanes = -(-need // 128) * 128
    piece = min(outs, lanes - taps * outs)
    return lanes, piece, places


def packed(conv_weights, zero_weights):
    blocks, convs, taps, depth, outs = conv_weights.shape
    channels = zero_weights.shape[2]
    lanes, piece, places = layout_of(conv_weights)
    main = jnp.transpose(conv_weights, (0, 1, 3, 2, 4)).reshape(blocks, convs, depth, taps * outs)
    zero = zero_weights[:, 0]
    zero = jnp.pad(zero, ((0, 0), (0, 0), (0, places * piece - outs)))
    zero = jnp.transpose(zero.reshape(blocks, channels, places, piece), (0, 2, 1, 3))
    zero = zero.reshape(blocks, convs, depth, piece)
    slab = jnp.concatenate([main, zero], axis=3)
    slab = jnp.pad(slab, ((0, 0), (0, 0), (0, 0), (0, lanes - slab.shape[3])))
    return slab.reshape(blocks * convs, depth, lanes)


def kernel(dims, x_ref, skip_ref, gain_ref, shift_ref, group_ref, w_ref, out_ref,
           slabs, wfull, zfull, stk, halo, fields, acc, stat_out, stat_in,
           z_send, z_recv, a_send, a_recv, b_send, b_recv, d_send, d_recv,
           h_send, h_recv, t_send, t_recv):
    rows_n, batch_n, height, across, channels, outs, taps, piece, members = dims
    convs, depth, lanes = w_ref.shape
    zn = batch_n // 2
    r = lax.axis_index("rows")
    b = lax.axis_index("batch")
    z, c = b // 2, b % 2
    bit0, bit1 = r % 2, (r // 2) % 2
    px, py = r + 1 - 2 * bit0, r + 2 - 4 * bit1
    p1 = (1 - c) * px + c * py
    p2 = (1 - c) * py + c * px
    q = (1 - c) * (2 * bit1 + bit0) + c * (2 * bit0 + bit1)
    mate = b + 1 - 2 * c
    quarter, half = depth // 4, depth // 2
    mine = pl.ds(pl.multiple_of(q * quarter, quarter), quarter)
    peer = pl.ds(pl.multiple_of((q + 1 - 2 * (q % 2)) * quarter, quarter), quarter)
    my_half = pl.ds(pl.multiple_of((q // 2) * half, half), half)
    other_half = pl.ds(pl.multiple_of((1 - q // 2) * half, half), half)
    order = sorted(range(1, zn), key=lambda j: min(j, zn - j))

    def remote(src, dst, send, recv, row, batch):
        return pltpu.make_async_remote_copy(
            src_ref=src, dst_ref=dst, send_sem=send, recv_sem=recv,
            device_id={"rows": row, "batch": batch}, device_id_type=MESH)

    barrier = pltpu.get_barrier_semaphore()
    for j in range(1, zn):
        pl.semaphore_signal(barrier, inc=1, device_id_type=MESH,
                            device_id={"rows": r, "batch": ((z + j) % zn) * 2 + c})
    for j in range(1, rows_n):
        pl.semaphore_signal(barrier, inc=1, device_id_type=MESH,
                            device_id={"rows": (r + j) % rows_n, "batch": b})
    pl.semaphore_signal(barrier, inc=1, device_id_type=MESH, device_id={"rows": r, "batch": mate})
    pl.semaphore_wait(barrier, zn + rows_n - 1)

    sent = []

    def start(copy):
        copy.start()
        sent.append(copy)

    def source(j):
        return ((z + zn - j) % zn) * 2 + c

    def z_start(k):
        for j in order:
            start(remote(w_ref.at[k, mine], slabs.at[k, b, mine], z_send.at[k, j], z_recv.at[k, j],
                         r, ((z + j) % zn) * 2 + c))

    def a_step(k):
        for j in order:
            s = source(j)
            here = slabs.at[k, s, mine]
            remote(here, here, z_send.at[k, j], z_recv.at[k, j], p1, b).wait_recv()
            start(remote(here, here, a_send.at[k, j], a_recv.at[k, j], p1, b))

    def b_step(k):
        for j in order:
            s = source(j)
            got = slabs.at[k, s, peer]
            remote(got, got, a_send.at[k, j], a_recv.at[k, j], p1, b).wait_recv()
            here = slabs.at[k, s, my_half]
            start(remote(here, here, b_send.at[k, j], b_recv.at[k, j], p2, b))

    def d_step(k):
        for j in order:
            s = source(j)
            got = slabs.at[k, s, other_half]
            remote(got, got, b_send.at[k, j], b_recv.at[k, j], p2, b).wait_recv()
            here = slabs.at[k, s]
            start(remote(here, here, d_send.at[k, j], d_recv.at[k, j], r, mate))

    def d_wait(k):
        for j in [0] + order:
            s = ((z + zn - j) % zn) * 2 + (1 - c)
            here = slabs.at[k, s]
            remote(here, here, d_send.at[k, j], d_recv.at[k, j], r, mate).wait_recv()

    chunk = channels // 2

    def assemble(k):
        def body(i, carry):
            at = pl.multiple_of(i * chunk, chunk)
            parts = [slabs[k, d, pl.ds(at, chunk), :] for d in range(batch_n)]
            for tap in range(taps):
                wfull[tap, pl.ds(at, chunk), :] = jnp.concatenate(
                    [part[:, tap * outs:(tap + 1) * outs] for part in parts], axis=1)
            return carry
        lax.fori_loop(0, depth // chunk, body, 0)

    def assemble_zero(block):
        per = depth // channels
        for top in range(0, channels, chunk):
            parts = []
            for d in range(batch_n):
                for place in range(-(-outs // piece)):
                    k = block * (convs // (convs // 2)) + place // per
                    at = (place % per) * channels + top
                    wide = min(piece, outs - place * piece)
                    parts.append(slabs[k, d, at:at + chunk, taps * outs:taps * outs + wide])
            zfull[top:top + chunk, :] = jnp.concatenate(parts, axis=1)

    def halo_start(s, ref):
        cells = height * across

        def down():
            return remote(ref.at[pl.ds(cells - across, across)], halo.at[s, 0],
                          h_send.at[s, 0], h_recv.at[s, 0], (r + 1) % rows_n, b)

        def up():
            return remote(ref.at[pl.ds(0, across)], halo.at[s, 1],
                          h_send.at[s, 1], h_recv.at[s, 1], (r + rows_n - 1) % rows_n, b)

        @pl.when(r < rows_n - 1)
        def _():
            down().start()

        @pl.when(r > 0)
        def _():
            up().start()

        return down, up

    def stat_start(s, values):
        total = jnp.sum(values, axis=0, keepdims=True)
        square = jnp.sum(values * values, axis=0, keepdims=True)
        stat_out[s] = jnp.concatenate([total, square, jnp.zeros((6, channels), jnp.float32)], axis=0)
        for j in range(1, rows_n):
            start(remote(stat_out.at[s], stat_in.at[s, j], t_send.at[s, j], t_recv.at[s, j],
                         (r + j) % rows_n, b))

    col = lax.broadcasted_iota(jnp.int32, (across, channels), 0)

    def normalize(s, ref, ends):
        total = stat_out[s]
        for j in range(1, rows_n):
            here = stat_in.at[s, j]
            remote(here, here, t_send.at[s, j], t_recv.at[s, j], r, mate).wait_recv()
            total = total + stat_in[s, j]
        grouped = jnp.dot(total, group_ref[...], precision=lax.Precision.HIGHEST,
                          preferred_element_type=jnp.float32) * (1.0 / members)
        mean = grouped[0:1]
        spread = jnp.maximum(grouped[1:2] - mean * mean, 0.0)
        scale = lax.rsqrt(spread + EPSILON) * gain_ref[s:s + 1, :]
        bias = shift_ref[s:s + 1, :] - mean * scale

        def put(at, v, valid):
            y = v.astype(jnp.float32) * scale + bias
            a = y / (1.0 + jnp.exp(-y))
            if valid is not None:
                a = jnp.where(valid, a, 0.0)
            left = jnp.where(col == 0, 0.0, pltpu.roll(a, 1, 0))
            right = jnp.where(col == across - 1, 0.0, pltpu.roll(a, across - 1, 0))
            stk[pl.ds(at, across), :] = jnp.concatenate(
                [left.astype(jnp.bfloat16), a.astype(jnp.bfloat16), right.astype(jnp.bfloat16)], axis=1)

        def body(i, carry):
            at = pl.multiple_of(i * across, across)
            put(pl.multiple_of(at + across, across), ref[pl.ds(at, across), :], None)
            return carry
        lax.fori_loop(0, height, body, 0)
        down, up = ends

        @pl.when(r > 0)
        def _():
            down().wait_recv()

        @pl.when(r < rows_n - 1)
        def _():
            up().wait_recv()

        put(0, halo[s, 0], r > 0)
        put((height + 1) * across, halo[s, 1], r < rows_n - 1)

    def convolve():
        cells = height * across
        for tap in range(taps):
            part = jnp.dot(stk[tap * across:tap * across + cells, :], wfull[tap],
                           preferred_element_type=jnp.float32)
            if tap == 0:
                acc[...] = part
            elif tap < taps - 1:
                acc[...] += part
            else:
                return acc[...] + part

    ends = [halo_start(0, x_ref)]
    for k in range(convs):
        z_start(k)
        start(remote(w_ref.at[k], slabs.at[k, b], d_send.at[k, 0], d_recv.at[k, 0], r, mate))
    stat_start(0, x_ref[...].astype(jnp.float32))
    for k in range(convs):
        slabs[k, b] = w_ref[k]
    a_step(0)
    normalize(0, x_ref, ends[0])
    b_step(0)
    a_step(1)
    d_step(0)
    b_step(1)
    source_ref = x_ref
    for s in range(convs):
        d_wait(s)
        assemble(s)
        if s > 0:
            normalize(s, fields.at[s - 1], ends[s])
        result = convolve()
        if s % 2 == 0:
            fields[s] = result.astype(jnp.bfloat16)
        else:
            fields[s] = (source_ref[...].astype(jnp.float32) + result).astype(jnp.bfloat16)
            source_ref = fields.at[s]
        if s < convs - 1:
            ends.append(halo_start(s + 1, fields.at[s]))
            stat_start(s + 1, fields[s].astype(jnp.float32))
        if s + 2 < convs:
            a_step(s + 2)
        if s + 1 < convs:
            d_step(s + 1)
        if s + 2 < convs:
            b_step(s + 2)
        if s % 2 == 1:
            block = s // 2
            assemble_zero(block)
            zeroed = jnp.dot(fields[s], zfull[...], preferred_element_type=jnp.float32)
            out_ref[block] = (skip_ref[block].astype(jnp.float32) + zeroed).astype(jnp.bfloat16)
    for copy in sent:
        copy.wait_send()
    for down, up in ends:
        @pl.when(r < rows_n - 1)
        def _():
            down().wait_send()

        @pl.when(r > 0)
        def _():
            up().wait_send()


def on_device(rows_n, batch_n, control, unet_skips, norm_gains, norm_shifts, conv_weights, zero_weights):
    blocks, convs, taps, depth, outs = conv_weights.shape
    samples, height, across, channels = control.shape
    lanes, piece, places = layout_of(conv_weights)
    stages = blocks * convs
    cells = height * across
    per = channels // GROUPS
    member = np.arange(channels) // per
    group = jnp.asarray((member[:, None] == member[None, :]).astype(np.float32))
    slab = packed(conv_weights, zero_weights)
    members = cells * rows_n * per
    dims = (rows_n, batch_n, height, across, channels, outs, taps, piece, members)
    zn = batch_n // 2
    dma = pltpu.SemaphoreType.DMA
    vmem = pl.BlockSpec(memory_space=pltpu.VMEM)
    out = pl.pallas_call(
        functools.partial(kernel, dims),
        out_shape=jax.ShapeDtypeStruct((blocks, cells, channels), jnp.bfloat16),
        in_specs=[vmem] * 6,
        out_specs=vmem,
        scratch_shapes=[
            pltpu.VMEM((stages, batch_n, depth, lanes), jnp.bfloat16),
            pltpu.VMEM((taps, depth, channels), jnp.bfloat16),
            pltpu.VMEM((channels, channels), jnp.bfloat16),
            pltpu.VMEM(((height + taps - 1) * across, depth), jnp.bfloat16),
            pltpu.VMEM((stages, 2, across, channels), jnp.bfloat16),
            pltpu.VMEM((stages, cells, channels), jnp.bfloat16),
            pltpu.VMEM((cells, channels), jnp.float32),
            pltpu.VMEM((stages, 8, channels), jnp.float32),
            pltpu.VMEM((stages, rows_n, 8, channels), jnp.float32),
            dma((stages, zn)), dma((stages, zn)),
            dma((stages, zn)), dma((stages, zn)),
            dma((stages, zn)), dma((stages, zn)),
            dma((stages, zn)), dma((stages, zn)),
            dma((stages, 2)), dma((stages, 2)),
            dma((stages, rows_n)), dma((stages, rows_n)),
        ],
        compiler_params=pltpu.CompilerParams(
            collective_id=0, has_side_effects=True, vmem_limit_bytes=50 * 1024 * 1024),
    )(
        control.reshape(cells, channels),
        unet_skips.reshape(blocks, cells, channels),
        norm_gains.reshape(stages, channels),
        norm_shifts.reshape(stages, channels),
        group,
        slab,
    )
    return out.reshape(blocks, samples, height, across, channels)


def solution(mesh):
    placed = (
        P("batch", "rows", None, None),
        P(None, "batch", "rows", None, None),
        P(),
        P(),
        P(None, None, None, None, "batch"),
        P(None, None, None, "batch"),
    )
    return jax.shard_map(
        functools.partial(on_device, mesh.shape["rows"], mesh.shape["batch"]),
        mesh=mesh,
        in_specs=placed,
        out_specs=P(None, "batch", "rows", None, None),
        check_vma=False,
    )
```

time: 154 us -> 76 us (0.49)
  blocking collectives: 73.5 us -> 0 us
  Pallas kernels: 0 us -> 69.1 us
  matrix products: 19.1 us -> 0 us
  waiting for transfers between devices: 15.9 us -> 0 us
  starting transfers between devices: 14.4 us -> 0 us
  between operations: 13.6 us -> 0.07 us
  local copies, waits for them, and re-layouts: 11.2 us -> 4.51 us
  other arithmetic: 5.14 us -> 2.17 us
    pallas_call x0 -> x1, Pallas kernels: none -> 69.1 us  [on_device(): pl.pallas_call(functools.partial(kernel, dims), out_shape=jax.ShapeDtypeS...]
    psum x4 -> x0, blocking collectives: 43.2 us -> none  [normalize(): lax.psum((jnp.sum(grouped, axis=(1, 2, 4), keepdims=True), jnp.sum(groupe...]
    all_gather x2 -> x0, blocking collectives: 30.3 us -> none  [convolve(): complete = lax.all_gather(weight, 'batch', axis=2, tiled=True)]
    dot_general x13 -> x0, matrix products: 19.1 us -> none  [apply_taps(): jnp.einsum('bhwk,kc->bhwc', stacked, weight_piece[row_tap], preferred_ele...]
    ppermute x8 -> x0, starting transfers between devices: 14.2 us -> none  [the longest x4 9.07 us: extended(): lax.ppermute(lax.slice_in_dim(block, block.shape[dim] - width, None, axis...]
    ppermute x8 -> x0, waiting for transfers between devices: 8.83 us -> none  [the longest x4 8.61 us: extended(): lax.ppermute(lax.slice_in_dim(block, 0, width, axis=dim), axis, backward)]
    slice x11 -> x0, local copies, waits for them, and re-layouts: 6.27 us -> none  [the longest x4 2.64 us: apply_taps(): row_band[:, :, col_tap:col_tap + across]]
    all_gather x4 -> x0, waiting for transfers between devices: 5.62 us -> none  [convolve(): complete = lax.all_gather(weight, 'batch', axis=2, tiled=True)]
  transfers between devices with their start and end apart: 12 -> 0, of which waited for: 4 -> 0; matrix products, arithmetic and copies ran while one was open for 14% -> 0% of each run, Pallas kernels for 0% -> 0%
where the time goes in v1:
time: 76 us; the launch traced here: 75.9 us
  Pallas kernels  69.1 us (91%)
  local copies, waits for them, and re-layouts  4.51 us (6%)
  other arithmetic  2.17 us (3%)
    pallas_call x1, Pallas kernels, on_device(): pl.pallas_call(functools.partial(kernel, dims), out_shape=jax.ShapeDtypeS...  69.1 us
    reshape x2, local copies, waits for them, and re-layouts, packed(): zero.reshape(blocks, channels, places, piece)  2.23 us
    concatenate x1, other arithmetic, packed(): slab = jnp.concatenate([main, zero], axis=3)  2.17 us

profile of v1, /device:TPU:0, one launch (start us, length us, event | category | flops | bytes accessed | tf_op | source)
XLA Modules:
  0.0 75.9 jit_solution(10270847043577282506)
XLA Ops:
  0.0 0.0 copy-start.3
  0.0 0.9 %pad_bitcast_fusion = bf16[2,320,6,8]{1,3,2,0:T(8,128)(2,1)S(1)} fusion(bf16[2,320,40]{1,2,0:T(8,128)(2,1)} %bitcast.19), kind=kLoop, calls=%fused_computation.1 | loop fusion | bytes 112640 | tf_op jit(solution)/shard_map/reshape | solution.py:33
  0.9 1.3 %copy.11 = bf16[2,320,6,8]{3,1,2,0:T(8,128)(2,1)} copy(bf16[2,320,6,8]{1,3,2,0:T(8,128)(2,1)S(1)} %pad_bitcast_fusion) | data formatting | bytes 122880 | tf_op jit(solution)/shard_map/reshape | solution.py:33
  2.2 0.0 copy-done.3
  2.2 1.3 %copy.12 = bf16[4,960,120]{2,1,0:T(8,128)(2,1)} copy(bf16[4,960,120]{1,2,0:T(8,128)(2,1)S(1)} %bitcast.18) | data formatting | bytes 1843200 | tf_op jit(solution)/shard_map/concatenate | solution.py:35
  3.5 0.0 copy-start.4
  3.6 0.0 copy-start.5
  3.6 0.0 copy-start
  3.6 0.0 copy-start.1
  3.6 0.0 copy-start.2
  3.6 2.2 %pad_maximum_fusion.w_ref = bf16[4,960,128]{2,1,0:T(8,128)(2,1)S(1)} fusion(bf16[4,960,8]{2,1,0:T(8,128)(2,1)} %bitcast.17, bf16[4,960,120]{2,1,0:T(8,128)(2,1)} %copy.12), kind=kLoop, calls=%fused_computation | loop fusion | flops 1966080 | bytes 1966080 | tf_op jit(solution)/shard_map/concatenate | solution.py:35
  5.7 0.0 copy-done.4
  5.8 0.0 copy-done.5
  5.8 0.0 copy-done
  5.8 0.0 copy-done.1
  5.8 0.0 copy-done.2
  5.8 69.1 %shard_map.73 = bf16[2,576,320]{2,1,0:T(8,128)(2,1)S(1)} custom-call(bf16[576,320]{1,0:T(8,128)(2,1)S(1)} %bitcast.16, bf16[2,576,320]{2,1,0:T(8,128)(2,1)S(1)} %bitcast.15, f32[4,320]{1,0:T(4,128)S(1)} %reshape.27.gain_ref, f32[4,320]{1,0:T(4,128)S(1)} %reshape.28.shift_ref, f32[320,320]{1,0:T(8,128)S(1)} %copy-done.1, ...), custom_call_target="tpu_custom_call" | custom-call | tf_op jit(solution)/shard_map/pallas_call | solution.py:295
  75.0 0.9 %copy.15 = bf16[2,1,6,96,320]{4,3,2,1,0:T(8,128)(2,1)} copy(bf16[2,1,6,96,320]{4,3,2,1,0:T(8,128)(2,1)S(1)} %bitcast.14) | data formatting | bytes 1474560
  (2 shorter events, 0.0 us)
Async XLA Ops:
  0.0 2.2 %copy-start.3 = (bf16[2,2,3,960,40]{3,4,2,1,0:T(8,128)(2,1)S(1)}, bf16[2,2,3,960,40]{3,4,2,1,0:T(8,128)(2,1)}, u32[]{:S(2)}) copy-start(bf16[2,2,3,960,40]{3,4,2,1,0:T(8,128)(2,1)} %param.11) | copy-start | bytes 2764804
  3.5 2.2 %copy-start.4 = (f32[2,2,320]{2,1,0:T(2,128)S(1)}, f32[2,2,320]{2,1,0:T(2,128)}, u32[]{:S(2)}) copy-start(f32[2,2,320]{2,1,0:T(2,128)} %param.9) | copy-start | bytes 15364
  3.6 2.2 %copy-start.5 = (f32[2,2,320]{2,1,0:T(2,128)S(1)}, f32[2,2,320]{2,1,0:T(2,128)}, u32[]{:S(2)}) copy-start(f32[2,2,320]{2,1,0:T(2,128)} %param.10) | copy-start | bytes 15364
  3.6 2.3 %copy-start = (bf16[2,1,6,96,320]{4,3,2,1,0:T(8,128)(2,1)S(1)}, bf16[2,1,6,96,320]{4,3,2,1,0:T(8,128)(2,1)}, u32[]{:S(2)}) copy-start(bf16[2,1,6,96,320]{4,3,2,1,0:T(8,128)(2,1)} %param.8) | copy-start | bytes 2211844
  3.6 2.3 %copy-start.1 = (f32[320,320]{1,0:T(8,128)S(1)}, f32[320,320]{1,0:T(8,128)}, u32[]{:S(2)}) copy-start(f32[320,320]{1,0:T(8,128)} %constant.5.clone.group_ref) | copy-start | bytes 1228804
  3.6 2.3 %copy-start.2 = (bf16[1,6,96,320]{3,2,1,0:T(8,128)(2,1)S(1)}, bf16[1,6,96,320]{3,2,1,0:T(8,128)(2,1)}, u32[]{:S(2)}) copy-start(bf16[1,6,96,320]{3,2,1,0:T(8,128)(2,1)} %param.7) | copy-start | bytes 1105924

commit v2 on v1

v2 whole, which is shorter than its diff:
```python
import functools

import jax
import jax.numpy as jnp
import numpy as np
from jax import lax
from jax.experimental import pallas as pl
from jax.experimental.pallas import tpu as pltpu
from jax.sharding import PartitionSpec as P

GROUPS = 32
EPSILON = 1e-05
MESH = pl.DeviceIdType.MESH


def transposed(conv_weights, zero_weights):
    blocks, convs, taps, depth, outs = conv_weights.shape
    conv = jnp.transpose(conv_weights, (0, 1, 2, 4, 3)).reshape(blocks * convs, taps * outs, depth)
    return conv, jnp.transpose(zero_weights[:, 0], (0, 2, 1))


def kernel(dims, x_ref, skip_ref, gain_ref, shift_ref, group_ref, w_ref, zw_ref, out_ref,
           slabs, wfull, zfull, stk, halo, fields, stat_out, stat_in,
           z_send, z_recv, a_send, a_recv, b_send, b_recv, d_send, d_recv,
           h_send, h_recv, t_send, t_recv):
    rows_n, batch_n, height, across, channels, outs, taps, members = dims
    convs, _, depth = w_ref.shape
    lanes = slabs.shape[3]
    piece = lanes - depth
    zn = batch_n // 2
    r = lax.axis_index("rows")
    b = lax.axis_index("batch")
    z, c = b // 2, b % 2
    bit0, bit1 = r % 2, (r // 2) % 2
    px, py = r + 1 - 2 * bit0, r + 2 - 4 * bit1
    p1 = (1 - c) * px + c * py
    p2 = (1 - c) * py + c * px
    q = (1 - c) * (2 * bit1 + bit0) + c * (2 * bit0 + bit1)
    mate = b + 1 - 2 * c
    quarter, half = lanes // 4, lanes // 2
    every = slice(None)
    mine = pl.ds(pl.multiple_of(q * quarter, quarter), quarter)
    peer = pl.ds(pl.multiple_of((q + 1 - 2 * (q % 2)) * quarter, quarter), quarter)
    my_half = pl.ds(pl.multiple_of((q // 2) * half, half), half)
    other_half = pl.ds(pl.multiple_of((1 - q // 2) * half, half), half)
    order = sorted(range(1, zn), key=lambda j: min(j, zn - j))

    def remote(src, dst, send, recv, row, batch):
        return pltpu.make_async_remote_copy(
            src_ref=src, dst_ref=dst, send_sem=send, recv_sem=recv,
            device_id={"rows": row, "batch": batch}, device_id_type=MESH)

    barrier = pltpu.get_barrier_semaphore()
    for j in range(1, zn):
        pl.semaphore_signal(barrier, inc=1, device_id_type=MESH,
                            device_id={"rows": r, "batch": ((z + j) % zn) * 2 + c})
    for j in range(1, rows_n):
        pl.semaphore_signal(barrier, inc=1, device_id_type=MESH,
                            device_id={"rows": (r + j) % rows_n, "batch": b})
    pl.semaphore_signal(barrier, inc=1, device_id_type=MESH, device_id={"rows": r, "batch": mate})

    pieces = -(-channels // piece)
    per_block = convs // zw_ref.shape[0]
    for k in range(convs):
        slabs[k, b, :, :depth] = w_ref[k]
        block = k // per_block
        for tap in range(taps):
            p = (k % per_block) * taps + tap
            if p < pieces:
                wide = min(piece, channels - p * piece)
                slabs[k, b, tap * outs:(tap + 1) * outs, depth:depth + wide] = (
                    zw_ref[block, :, p * piece:p * piece + wide])
    pl.semaphore_wait(barrier, zn + rows_n - 1)

    sent = []

    def start(copy):
        copy.start()
        sent.append(copy)

    def source(j):
        return ((z + zn - j) % zn) * 2 + c

    def z_start(k):
        here = slabs.at[k, b, every, mine]
        for j in order:
            start(remote(here, here, z_send.at[k, j], z_recv.at[k, j],
                         r, ((z + j) % zn) * 2 + c))

    def a_step(k):
        for j in order:
            s = source(j)
            here = slabs.at[k, s, every, mine]
            remote(here, here, z_send.at[k, j], z_recv.at[k, j], p1, b).wait_recv()
            start(remote(here, here, a_send.at[k, j], a_recv.at[k, j], p1, b))

    def b_step(k):
        for j in order:
            s = source(j)
            got = slabs.at[k, s, every, peer]
            remote(got, got, a_send.at[k, j], a_recv.at[k, j], p1, b).wait_recv()
            here = slabs.at[k, s, every, my_half]
            start(remote(here, here, b_send.at[k, j], b_recv.at[k, j], p2, b))

    def d_step(k):
        for j in order:
            s = source(j)
            got = slabs.at[k, s, every, other_half]
            remote(got, got, b_send.at[k, j], b_recv.at[k, j], p2, b).wait_recv()
            here = slabs.at[k, s]
            start(remote(here, here, d_send.at[k, j], d_recv.at[k, j], r, mate))

    def d_wait(k):
        for j in [0] + order:
            s = ((z + zn - j) % zn) * 2 + (1 - c)
            here = slabs.at[k, s]
            remote(here, here, d_send.at[k, j], d_recv.at[k, j], r, mate).wait_recv()

    def assemble(k):
        for d in range(batch_n):
            for tap in range(taps):
                wfull[tap, d * outs:(d + 1) * outs, :] = (
                    slabs[k, d, tap * outs:(tap + 1) * outs, :depth])

    def assemble_zero(block):
        for d in range(batch_n):
            parts = []
            for p in range(pieces):
                wide = min(piece, channels - p * piece)
                tap = p % taps
                parts.append(slabs[block * per_block + p // taps, d,
                                   tap * outs:(tap + 1) * outs, depth:depth + wide])
            zfull[d * outs:(d + 1) * outs, :] = jnp.concatenate(parts, axis=1)

    def times(a, w):
        return lax.dot_general(a, w, (((1,), (1,)), ((), ())), preferred_element_type=jnp.float32)

    def halo_start(s, ref):
        cells = height * across

        def down():
            return remote(ref.at[pl.ds(cells - across, across)], halo.at[s, 0],
                          h_send.at[s, 0], h_recv.at[s, 0], (r + 1) % rows_n, b)

        def up():
            return remote(ref.at[pl.ds(0, across)], halo.at[s, 1],
                          h_send.at[s, 1], h_recv.at[s, 1], (r + rows_n - 1) % rows_n, b)

        @pl.when(r < rows_n - 1)
        def _():
            down().start()

        @pl.when(r > 0)
        def _():
            up().start()

        return down, up

    def stat_start(s, total, square):
        stat_out[s] = jnp.concatenate([total, square, jnp.zeros((6, channels), jnp.float32)], axis=0)
        for j in range(1, rows_n):
            start(remote(stat_out.at[s], stat_in.at[s, j], t_send.at[s, j], t_recv.at[s, j],
                         (r + j) % rows_n, b))

    col = lax.broadcasted_iota(jnp.int32, (across, channels), 0)

    def normalize(s, ref):
        total = stat_out[s]
        for j in range(1, rows_n):
            here = stat_in.at[s, j]
            remote(here, here, t_send.at[s, j], t_recv.at[s, j], r, mate).wait_recv()
            total = total + stat_in[s, j]
        grouped = jnp.dot(total, group_ref[...], precision=lax.Precision.HIGHEST,
                          preferred_element_type=jnp.float32) * (1.0 / members)
        mean = grouped[0:1]
        spread = jnp.maximum(grouped[1:2] - mean * mean, 0.0)
        scale = lax.rsqrt(spread + EPSILON) * gain_ref[s:s + 1, :]
        bias = shift_ref[s:s + 1, :] - mean * scale

        def put(at, v, valid):
            y = v.astype(jnp.float32) * scale + bias
            a = y / (1.0 + jnp.exp(-y))
            if valid is not None:
                a = jnp.where(valid, a, 0.0)
            left = jnp.where(col == 0, 0.0, pltpu.roll(a, 1, 0))
            right = jnp.where(col == across - 1, 0.0, pltpu.roll(a, across - 1, 0))
            stk[pl.ds(at, across), :] = jnp.concatenate(
                [left.astype(jnp.bfloat16), a.astype(jnp.bfloat16), right.astype(jnp.bfloat16)], axis=1)

        def body(i, carry):
            at = pl.multiple_of(i * across, across)
            put(pl.multiple_of(at + across, across), ref[pl.ds(at, across), :], None)
            return carry
        lax.fori_loop(0, height, body, 0)
        return put

    def edges(s, put, ends):
        down, up = ends

        @pl.when(r > 0)
        def _():
            down().wait_recv()

        @pl.when(r < rows_n - 1)
        def _():
            up().wait_recv()

        put(0, halo[s, 0], r > 0)
        put((height + 1) * across, halo[s, 1], r < rows_n - 1)

    def inner():
        cells = (height - 2) * across
        total = None
        for tap in range(taps):
            at = (tap + 1) * across
            part = times(stk[at:at + cells, :], wfull[tap])
            total = part if total is None else total + part
        return total

    def outer():
        total = None
        for tap in range(taps):
            low, high = tap * across, (height - 1 + tap) * across
            both = jnp.concatenate([stk[low:low + across, :], stk[high:high + across, :]], axis=0)
            part = times(both, wfull[tap])
            total = part if total is None else total + part
        return total

    def convolve(s, put, ends, source):
        cells = height * across

        def keep(at, value):
            size = value.shape[0]
            if source is not None:
                value = source[at:at + size, :].astype(jnp.float32) + value
            value = value.astype(jnp.bfloat16)
            fields[s, at:at + size, :] = value
            kept = value.astype(jnp.float32)
            return (jnp.sum(kept, axis=0, keepdims=True),
                    jnp.sum(kept * kept, axis=0, keepdims=True))

        middle = keep(across, inner())
        edges(s, put, ends)
        border = outer()
        top = keep(0, border[:across])
        bottom = keep(cells - across, border[across:])
        return middle[0] + top[0] + bottom[0], middle[1] + top[1] + bottom[1]

    def zero_conv(s):
        block = s // per_block
        assemble_zero(block)
        zeroed = times(fields[s], zfull[...])
        out_ref[block] = (skip_ref[block].astype(jnp.float32) + zeroed).astype(jnp.bfloat16)

    ends = [halo_start(0, x_ref)]
    for k in range(convs):
        z_start(k)
        here = slabs.at[k, b]
        start(remote(here, here, d_send.at[k, 0], d_recv.at[k, 0], r, mate))
        if k == 0:
            first = x_ref[...].astype(jnp.float32)
            stat_start(0, jnp.sum(first, axis=0, keepdims=True),
                       jnp.sum(first * first, axis=0, keepdims=True))
    put = normalize(0, x_ref)
    a_step(0)
    b_step(0)
    a_step(1)
    d_step(0)
    b_step(1)
    source_ref = x_ref
    for s in range(convs):
        d_wait(s)
        assemble(s)
        if s + 2 < convs:
            a_step(s + 2)
        if s > 0:
            put = normalize(s, fields.at[s - 1])
        last = s % per_block == per_block - 1
        sums = convolve(s, put, ends[s], source_ref if last else None)
        if last:
            source_ref = fields.at[s]
        if s < convs - 1:
            stat_start(s + 1, *sums)
            ends.append(halo_start(s + 1, fields.at[s]))
        if s + 1 < convs:
            d_step(s + 1)
        if s + 2 < convs:
            b_step(s + 2)
        if last:
            zero_conv(s)
    for copy in sent:
        copy.wait_send()
    for down, up in ends:
        @pl.when(r < rows_n - 1)
        def _():
            down().wait_send()

        @pl.when(r > 0)
        def _():
            up().wait_send()


def on_device(rows_n, batch_n, control, unet_skips, norm_gains, norm_shifts, conv_weights, zero_weights):
    blocks, convs, taps, depth, outs = conv_weights.shape
    samples, height, across, channels = control.shape
    lanes = (depth // 512 + 1) * 512
    stages = blocks * convs
    cells = height * across
    per = channels // GROUPS
    member = np.arange(channels) // per
    group = jnp.asarray((member[:, None] == member[None, :]).astype(np.float32))
    conv, zero = transposed(conv_weights, zero_weights)
    members = cells * rows_n * per
    dims = (rows_n, batch_n, height, across, channels, outs, taps, members)
    zn = batch_n // 2
    dma = pltpu.SemaphoreType.DMA
    vmem = pl.BlockSpec(memory_space=pltpu.VMEM)
    out = pl.pallas_call(
        functools.partial(kernel, dims),
        out_shape=jax.ShapeDtypeStruct((blocks, cells, channels), jnp.bfloat16),
        in_specs=[vmem] * 7,
        out_specs=vmem,
        scratch_shapes=[
            pltpu.VMEM((stages, batch_n, taps * outs, lanes), jnp.bfloat16),
            pltpu.VMEM((taps, channels, depth), jnp.bfloat16),
            pltpu.VMEM((channels, channels), jnp.bfloat16),
            pltpu.VMEM(((height + taps - 1) * across, depth), jnp.bfloat16),
            pltpu.VMEM((stages, 2, across, channels), jnp.bfloat16),
            pltpu.VMEM((stages, cells, channels), jnp.bfloat16),
            pltpu.VMEM((stages, 8, channels), jnp.float32),
            pltpu.VMEM((stages, rows_n, 8, channels), jnp.float32),
            dma((stages, zn)), dma((stages, zn)),
            dma((stages, zn)), dma((stages, zn)),
            dma((stages, zn)), dma((stages, zn)),
            dma((stages, zn)), dma((stages, zn)),
            dma((stages, 2)), dma((stages, 2)),
            dma((stages, rows_n)), dma((stages, rows_n)),
        ],
        compiler_params=pltpu.CompilerParams(
            collective_id=0, has_side_effects=True, vmem_limit_bytes=50 * 1024 * 1024),
    )(
        control.reshape(cells, channels),
        unet_skips.reshape(blocks, cells, channels),
        norm_gains.reshape(stages, channels),
        norm_shifts.reshape(stages, channels),
        group,
        conv,
        zero,
    )
    return out.reshape(blocks, samples, height, across, channels)


def solution(mesh):
    placed = (
        P("batch", "rows", None, None),
        P(None, "batch", "rows", None, None),
        P(),
        P(),
        P(None, None, None, None, "batch"),
        P(None, None, None, "batch"),
    )
    return jax.shard_map(
        functools.partial(on_device, mesh.shape["rows"], mesh.shape["batch"]),
        mesh=mesh,
        in_specs=placed,
        out_specs=P(None, "batch", "rows", None, None),
        check_vma=False,
    )
```

time: 76 us -> 64.5 us (0.85)
  Pallas kernels: 69.1 us -> 56.5 us
  local copies, waits for them, and re-layouts: 4.51 us -> 7.54 us
  other arithmetic: 2.17 us -> 0 us
    pallas_call x1, Pallas kernels: 69.1 us -> 56.5 us  [on_device(): pl.pallas_call(functools.partial(kernel, dims), out_shape=jax.ShapeDtypeS...]
    unnamed x13 -> x15, local copies, waits for them, and re-layouts: 0.94 us -> 7.51 us
    reshape x2 -> x0, local copies, waits for them, and re-layouts: 2.23 us -> none  [packed(): zero.reshape(blocks, channels, places, piece)]
    concatenate x1 -> x0, other arithmetic: 2.17 us -> none  [packed(): slab = jnp.concatenate([main, zero], axis=3)]
    concatenate x1 -> x0, local copies, waits for them, and re-layouts: 1.31 us -> none  [packed(): slab = jnp.concatenate([main, zero], axis=3)]
where the time goes in v2:
time: 64.5 us; the launch traced here: 64.1 us
  Pallas kernels  56.5 us (88%)
  local copies, waits for them, and re-layouts  7.54 us (12%)
    pallas_call x1, Pallas kernels, on_device(): pl.pallas_call(functools.partial(kernel, dims), out_shape=jax.ShapeDtypeS...  56.5 us
    unnamed x15, local copies, waits for them, and re-layouts  7.51 us

profile of v2, /device:TPU:0, one launch (start us, length us, event | category | flops | bytes accessed | tf_op | source)
XLA Modules:
  0.0 64.1 jit_solution(8235109225513479079)
XLA Ops:
  0.0 0.0 copy-start.5
  0.0 0.7 %copy-done.5 = f32[2,2,320]{2,1,0:T(2,128)S(1)} copy-done((f32[2,2,320]{2,1,0:T(2,128)S(1)}, f32[2,2,320]{2,1,0:T(2,128)}, u32[]{:S(2)}) %copy-start.5) | copy-done | bytes 5144
  0.7 0.0 copy-start.6
  0.7 0.7 %copy-done.6 = f32[2,2,320]{2,1,0:T(2,128)S(1)} copy-done((f32[2,2,320]{2,1,0:T(2,128)S(1)}, f32[2,2,320]{2,1,0:T(2,128)}, u32[]{:S(2)}) %copy-start.6) | copy-done | bytes 5144
  1.4 0.0 copy-start
  1.4 1.2 %copy-done = bf16[2,2,3,960,40]{3,4,2,1,0:T(8,128)(2,1)S(1)} copy-done((bf16[2,2,3,960,40]{3,4,2,1,0:T(8,128)(2,1)S(1)}, bf16[2,2,3,960,40]{3,4,2,1,0:T(8,128)(2,1)}, u32[]{:S(2)}) %copy-start) | copy-done | bytes 921624
  2.6 0.0 copy-start.1
  2.6 1.2 %copy-done.1 = bf16[2,1,6,96,320]{4,3,2,1,0:T(8,128)(2,1)S(1)} copy-done((bf16[2,1,6,96,320]{4,3,2,1,0:T(8,128)(2,1)S(1)}, bf16[2,1,6,96,320]{4,3,2,1,0:T(8,128)(2,1)}, u32[]{:S(2)}) %copy-start.1) | copy-done | bytes 737304
  3.8 0.0 copy-start.2
  3.8 1.0 %copy-done.2 = f32[320,320]{1,0:T(8,128)S(1)} copy-done((f32[320,320]{1,0:T(8,128)S(1)}, f32[320,320]{1,0:T(8,128)}, u32[]{:S(2)}) %copy-start.2) | copy-done | bytes 409624
  4.8 0.0 copy-start.3
  4.8 1.0 %copy-done.3 = bf16[1,6,96,320]{3,2,1,0:T(8,128)(2,1)S(1)} copy-done((bf16[1,6,96,320]{3,2,1,0:T(8,128)(2,1)S(1)}, bf16[1,6,96,320]{3,2,1,0:T(8,128)(2,1)}, u32[]{:S(2)}) %copy-start.3) | copy-done | bytes 368664
  5.8 0.0 copy-start.4
  5.8 0.8 %copy-done.4 = bf16[2,1,320,40]{2,3,1,0:T(8,128)(2,1)S(1)} copy-done((bf16[2,1,320,40]{2,3,1,0:T(8,128)(2,1)S(1)}, bf16[2,1,320,40]{2,3,1,0:T(8,128)(2,1)}, u32[]{:S(2)}) %copy-start.4) | copy-done | bytes 51224
  6.6 56.5 %shard_map.73 = bf16[2,576,320]{2,1,0:T(8,128)(2,1)S(1)} custom-call(bf16[576,320]{1,0:T(8,128)(2,1)S(1)} %bitcast.14, bf16[2,576,320]{2,1,0:T(8,128)(2,1)S(1)} %bitcast.13, f32[4,320]{1,0:T(4,128)S(1)} %reshape.20.gain_ref, f32[4,320]{1,0:T(4,128)S(1)} %reshape.21.shift_ref, f32[320,320]{1,0:T(8,128)S(1)} %copy-done.2, bf16[4,120,960]{2,1,0:T(8,128)(2,1)S(1)} %bitcast.12, ...), custom_call_target="tpu_custom_call" | custom-call | tf_op jit(solution)/shard_map/pallas_call | solution.py:318
  63.2 0.9 %copy.10 = bf16[2,1,6,96,320]{4,3,2,1,0:T(8,128)(2,1)} copy(bf16[2,1,6,96,320]{4,3,2,1,0:T(8,128)(2,1)S(1)} %bitcast.11) | data formatting | bytes 1474560
  (2 shorter events, 0.0 us)
Async XLA Ops:
  0.0 0.7 %copy-start.5 = (f32[2,2,320]{2,1,0:T(2,128)S(1)}, f32[2,2,320]{2,1,0:T(2,128)}, u32[]{:S(2)}) copy-start(f32[2,2,320]{2,1,0:T(2,128)} %param.9) | copy-start | bytes 15364
  0.7 0.7 %copy-start.6 = (f32[2,2,320]{2,1,0:T(2,128)S(1)}, f32[2,2,320]{2,1,0:T(2,128)}, u32[]{:S(2)}) copy-start(f32[2,2,320]{2,1,0:T(2,128)} %param.10) | copy-start | bytes 15364
  1.4 1.2 %copy-start = (bf16[2,2,3,960,40]{3,4,2,1,0:T(8,128)(2,1)S(1)}, bf16[2,2,3,960,40]{3,4,2,1,0:T(8,128)(2,1)}, u32[]{:S(2)}) copy-start(bf16[2,2,3,960,40]{3,4,2,1,0:T(8,128)(2,1)} %param.11) | copy-start | bytes 2764804
  2.6 1.2 %copy-start.1 = (bf16[2,1,6,96,320]{4,3,2,1,0:T(8,128)(2,1)S(1)}, bf16[2,1,6,96,320]{4,3,2,1,0:T(8,128)(2,1)}, u32[]{:S(2)}) copy-start(bf16[2,1,6,96,320]{4,3,2,1,0:T(8,128)(2,1)} %param.8) | copy-start | bytes 2211844
  3.8 1.0 %copy-start.2 = (f32[320,320]{1,0:T(8,128)S(1)}, f32[320,320]{1,0:T(8,128)}, u32[]{:S(2)}) copy-start(f32[320,320]{1,0:T(8,128)} %constant.2.clone.group_ref) | copy-start | bytes 1228804
  4.8 1.0 %copy-start.3 = (bf16[1,6,96,320]{3,2,1,0:T(8,128)(2,1)S(1)}, bf16[1,6,96,320]{3,2,1,0:T(8,128)(2,1)}, u32[]{:S(2)}) copy-start(bf16[1,6,96,320]{3,2,1,0:T(8,128)(2,1)} %param.7) | copy-start | bytes 1105924
  5.8 0.8 %copy-start.4 = (bf16[2,1,320,40]{2,3,1,0:T(8,128)(2,1)S(1)}, bf16[2,1,320,40]{2,3,1,0:T(8,128)(2,1)}, u32[]{:S(2)}) copy-start(bf16[2,1,320,40]{2,3,1,0:T(8,128)(2,1)} %param.12) | copy-start | bytes 153604

commit v3 on v2

--- a/solution.py
+++ b/solution.py
@@ -19,12 +19,18 @@
     return conv, jnp.transpose(zero_weights[:, 0], (0, 2, 1))
 
 
-def kernel(dims, x_ref, skip_ref, gain_ref, shift_ref, group_ref, w_ref, zw_ref, out_ref,
+def kernel(dims, x_far, skip_far, gain_far, shift_far, group_far, w_far, zw_far, out_ref,
+           x_ref, skip_ref, gain_ref, shift_ref, group_ref, w_ref, zw_ref, near_sem,
            slabs, wfull, zfull, stk, halo, fields, stat_out, stat_in,
            z_send, z_recv, a_send, a_recv, b_send, b_recv, d_send, d_recv,
            h_send, h_recv, t_send, t_recv):
     rows_n, batch_n, height, across, channels, outs, taps, members = dims
     convs, _, depth = w_ref.shape
+    loads = [pltpu.make_async_copy(far, close, near_sem.at[i]) for i, (far, close) in enumerate((
+        (w_far, w_ref), (zw_far, zw_ref), (x_far, x_ref), (gain_far, gain_ref),
+        (shift_far, shift_ref), (group_far, group_ref), (skip_far, skip_ref)))]
+    for load in loads:
+        load.start()
     lanes = slabs.shape[3]
     piece = lanes - depth
     zn = batch_n // 2
@@ -59,6 +65,8 @@
                             device_id={"rows": (r + j) % rows_n, "batch": b})
     pl.semaphore_signal(barrier, inc=1, device_id_type=MESH, device_id={"rows": r, "batch": mate})
 
+    for load in loads[:-1]:
+        load.wait()
     pieces = -(-channels // piece)
     per_block = convs // zw_ref.shape[0]
     for k in range(convs):
@@ -174,8 +182,8 @@
                           preferred_element_type=jnp.float32) * (1.0 / members)
         mean = grouped[0:1]
         spread = jnp.maximum(grouped[1:2] - mean * mean, 0.0)
-        scale = lax.rsqrt(spread + EPSILON) * gain_ref[s:s + 1, :]
-        bias = shift_ref[s:s + 1, :] - mean * scale
+        scale = lax.rsqrt(spread + EPSILON) * gain_ref[s // per_block, s % per_block:s % per_block + 1, :]
+        bias = shift_ref[s // per_block, s % per_block:s % per_block + 1, :] - mean * scale
 
         def put(at, v, valid):
             y = v.astype(jnp.float32) * scale + bias
@@ -267,6 +275,7 @@
     a_step(1)
     d_step(0)
     b_step(1)
+    loads[-1].wait()
     source_ref = x_ref
     for s in range(convs):
         d_wait(s)
@@ -318,9 +327,17 @@
     out = pl.pallas_call(
         functools.partial(kernel, dims),
         out_shape=jax.ShapeDtypeStruct((blocks, cells, channels), jnp.bfloat16),
-        in_specs=[vmem] * 7,
+        in_specs=[pl.BlockSpec(memory_space=pltpu.HBM)] * 7,
         out_specs=vmem,
         scratch_shapes=[
+            pltpu.VMEM((cells, channels), jnp.bfloat16),
+            pltpu.VMEM((blocks, cells, channels), jnp.bfloat16),
+            pltpu.VMEM(norm_gains.shape, jnp.float32),
+            pltpu.VMEM(norm_shifts.shape, jnp.float32),
+            pltpu.VMEM(group.shape, jnp.float32),
+            pltpu.VMEM(conv.shape, jnp.bfloat16),
+            pltpu.VMEM(zero.shape, jnp.bfloat16),
+            dma((7,)),
             pltpu.VMEM((stages, batch_n, taps * outs, lanes), jnp.bfloat16),
             pltpu.VMEM((taps, channels, depth), jnp.bfloat16),
             pltpu.VMEM((channels, channels), jnp.bfloat16),
@@ -341,8 +358,8 @@
     )(
         control.reshape(cells, channels),
         unet_skips.reshape(blocks, cells, channels),
-        norm_gains.reshape(stages, channels),
-        norm_shifts.reshape(stages, channels),
+        norm_gains,
+        norm_shifts,
         group,
         conv,
         zero,

time: 64.5 us -> 65.9 us (1.022)
  Pallas kernels: 56.5 us -> 58 us
    pallas_call x1, Pallas kernels: 56.5 us -> 58 us  [on_device(): pl.pallas_call(functools.partial(kernel, dims), out_shape=jax.ShapeDtypeS...]
where the time goes in v3:
time: 65.9 us; the launch traced here: 65.5 us
  Pallas kernels  58 us (88%)
  local copies, waits for them, and re-layouts  7.53 us (11%)
    pallas_call x1, Pallas kernels, on_device(): pl.pallas_call(functools.partial(kernel, dims), out_shape=jax.ShapeDtypeS...  58 us
    unnamed x15, local copies, waits for them, and re-layouts  7.53 us

profile of v3, /device:TPU:0, one launch (start us, length us, event | category | flops | bytes accessed | tf_op | source)
XLA Modules:
  0.0 65.5 jit_solution(14043694186313481075)
XLA Ops:
  0.0 0.0 copy-start.5
  0.0 0.7 %copy-done.5 = f32[2,2,320]{2,1,0:T(2,128)S(1)} copy-done((f32[2,2,320]{2,1,0:T(2,128)S(1)}, f32[2,2,320]{2,1,0:T(2,128)}, u32[]{:S(2)}) %copy-start.5) | copy-done | bytes 5144
  0.7 0.0 copy-start
  0.7 1.2 %copy-done = bf16[2,2,3,960,40]{3,4,2,1,0:T(8,128)(2,1)S(1)} copy-done((bf16[2,2,3,960,40]{3,4,2,1,0:T(8,128)(2,1)S(1)}, bf16[2,2,3,960,40]{3,4,2,1,0:T(8,128)(2,1)}, u32[]{:S(2)}) %copy-start) | copy-done | bytes 921624
  1.9 0.0 copy-start.1
  1.9 1.2 %copy-done.1 = bf16[2,1,6,96,320]{4,3,2,1,0:T(8,128)(2,1)S(1)} copy-done((bf16[2,1,6,96,320]{4,3,2,1,0:T(8,128)(2,1)S(1)}, bf16[2,1,6,96,320]{4,3,2,1,0:T(8,128)(2,1)}, u32[]{:S(2)}) %copy-start.1) | copy-done | bytes 737304
  3.1 0.0 copy-start.2
  3.1 1.0 %copy-done.2 = f32[320,320]{1,0:T(8,128)S(1)} copy-done((f32[320,320]{1,0:T(8,128)S(1)}, f32[320,320]{1,0:T(8,128)}, u32[]{:S(2)}) %copy-start.2) | copy-done | bytes 409624
  4.1 0.0 copy-start.3
  4.1 1.0 %copy-done.3 = bf16[1,6,96,320]{3,2,1,0:T(8,128)(2,1)S(1)} copy-done((bf16[1,6,96,320]{3,2,1,0:T(8,128)(2,1)S(1)}, bf16[1,6,96,320]{3,2,1,0:T(8,128)(2,1)}, u32[]{:S(2)}) %copy-start.3) | copy-done | bytes 368664
  5.1 0.0 copy-start.4
  5.1 0.8 %copy-done.4 = bf16[2,1,320,40]{2,3,1,0:T(8,128)(2,1)S(1)} copy-done((bf16[2,1,320,40]{2,3,1,0:T(8,128)(2,1)S(1)}, bf16[2,1,320,40]{2,3,1,0:T(8,128)(2,1)}, u32[]{:S(2)}) %copy-start.4) | copy-done | bytes 51224
  5.9 0.0 copy-start.6
  5.9 0.7 %copy-done.6 = f32[2,2,320]{2,1,0:T(2,128)S(1)} copy-done((f32[2,2,320]{2,1,0:T(2,128)S(1)}, f32[2,2,320]{2,1,0:T(2,128)}, u32[]{:S(2)}) %copy-start.6) | copy-done | bytes 5144
  6.6 58.0 %shard_map.73 = bf16[2,576,320]{2,1,0:T(8,128)(2,1)S(1)} custom-call(bf16[576,320]{1,0:T(8,128)(2,1)S(1)} %bitcast.14, bf16[2,576,320]{2,1,0:T(8,128)(2,1)S(1)} %bitcast.13, f32[2,2,320]{2,1,0:T(2,128)S(1)} %copy-done.5, f32[2,2,320]{2,1,0:T(2,128)S(1)} %copy-done.6, f32[320,320]{1,0:T(8,128)S(1)} %copy-done.2, bf16[4,120,960]{2,1,0:T(8,128)(2,1)S(1)} %bitcast.12, ...), custom_call_target="tpu_custom_call" | custom-call | tf_op jit(solution)/shard_map/pallas_call | solution.py:327
  64.6 0.9 %copy.10 = bf16[2,1,6,96,320]{4,3,2,1,0:T(8,128)(2,1)} copy(bf16[2,1,6,96,320]{4,3,2,1,0:T(8,128)(2,1)S(1)} %bitcast.11) | data formatting | bytes 1474560
Async XLA Ops:
  0.0 0.7 %copy-start.5 = (f32[2,2,320]{2,1,0:T(2,128)S(1)}, f32[2,2,320]{2,1,0:T(2,128)}, u32[]{:S(2)}) copy-start(f32[2,2,320]{2,1,0:T(2,128)} %gain_far.1) | copy-start | bytes 15364
  0.7 1.2 %copy-start = (bf16[2,2,3,960,40]{3,4,2,1,0:T(8,128)(2,1)S(1)}, bf16[2,2,3,960,40]{3,4,2,1,0:T(8,128)(2,1)}, u32[]{:S(2)}) copy-start(bf16[2,2,3,960,40]{3,4,2,1,0:T(8,128)(2,1)} %param.11) | copy-start | bytes 2764804
  1.9 1.2 %copy-start.1 = (bf16[2,1,6,96,320]{4,3,2,1,0:T(8,128)(2,1)S(1)}, bf16[2,1,6,96,320]{4,3,2,1,0:T(8,128)(2,1)}, u32[]{:S(2)}) copy-start(bf16[2,1,6,96,320]{4,3,2,1,0:T(8,128)(2,1)} %param.8) | copy-start | bytes 2211844
  3.1 1.0 %copy-start.2 = (f32[320,320]{1,0:T(8,128)S(1)}, f32[320,320]{1,0:T(8,128)}, u32[]{:S(2)}) copy-start(f32[320,320]{1,0:T(8,128)} %constant.2.clone.group_far) | copy-start | bytes 1228804
  4.1 1.0 %copy-start.3 = (bf16[1,6,96,320]{3,2,1,0:T(8,128)(2,1)S(1)}, bf16[1,6,96,320]{3,2,1,0:T(8,128)(2,1)}, u32[]{:S(2)}) copy-start(bf16[1,6,96,320]{3,2,1,0:T(8,128)(2,1)} %param.7) | copy-start | bytes 1105924
  5.1 0.8 %copy-start.4 = (bf16[2,1,320,40]{2,3,1,0:T(8,128)(2,1)S(1)}, bf16[2,1,320,40]{2,3,1,0:T(8,128)(2,1)}, u32[]{:S(2)}) copy-start(bf16[2,1,320,40]{2,3,1,0:T(8,128)(2,1)} %param.12) | copy-start | bytes 153604
  5.9 0.7 %copy-start.6 = (f32[2,2,320]{2,1,0:T(2,128)S(1)}, f32[2,2,320]{2,1,0:T(2,128)}, u32[]{:S(2)}) copy-start(f32[2,2,320]{2,1,0:T(2,128)} %shift_far.1) | copy-start | bytes 15364
